TPU v7x, 32 devices: a whole 2x2x4 slice. The times are simulated.
32 devices in a mesh: dp: 16 (over z, y, x), mp: 2 (over core).
Axes of the slice: x: 2, y: 2, z: 4, core: 2. Of those that a mesh axis runs over, the one named last changes fastest.
Arguments:
- hidden_state: bfloat16 [32, 19, 19, 256], P('dp'), may hold values from -6 to 6
- actions: int32 [32, 2], P('dp'), may hold values from 0 to 361
- value_target: int32 [32, 2], P('dp'), may hold values from 0 to 600
- reward_target: int32 [32, 2], P('dp'), may hold values from 0 to 600
- kernel_first: float32 [3, 3, 256, 256], P(None, None, 'dp', 'mp'), may hold values from -6 to 6
- kernel_second: float32 [3, 3, 256, 256], P(None, None, 'dp', 'mp'), may hold values from -6 to 6
- head_weight: float32 [2, 256, 601], P('mp', 'dp'), may hold values from -6 to 6
- action_embed: float32 [2, 256], P('mp', 'dp'), may hold values from -6 to 6
- first_mean: float32 [3, 3, 256, 256], P(None, None, 'dp', 'mp'), may hold values from -0.00061035156 to 0.00061035156
- first_square: float32 [3, 3, 256, 256], P(None, None, 'dp', 'mp'), may hold values from 1e-09 to 1e-06
- second_mean: float32 [3, 3, 256, 256], P(None, None, 'dp', 'mp'), may hold values from -0.00061035156 to 0.00061035156
- second_square: float32 [3, 3, 256, 256], P(None, None, 'dp', 'mp'), may hold values from 1e-09 to 1e-06
- head_mean: float32 [2, 256, 601], P('mp', 'dp'), may hold values from -0.0029296875 to 0.0029296875
- head_square: float32 [2, 256, 601], P('mp', 'dp'), may hold values from 1e-08 to 1e-06
- embed_mean: float32 [2, 256], P('mp', 'dp'), may hold values from -0.0017089844 to 0.0017089844
- embed_square: float32 [2, 256], P('mp', 'dp'), may hold values from 1e-09 to 1e-06
Outputs:
- kernel_first_new: float32 [3, 3, 256, 256], P(None, None, 'dp', 'mp')
- kernel_second_new: float32 [3, 3, 256, 256], P(None, None, 'dp', 'mp')
- head_weight_new: float32 [2, 256, 601], P('mp', 'dp')
- action_embed_new: float32 [2, 256], P('mp', 'dp')
- first_mean_new: float32 [3, 3, 256, 256], P(None, None, 'dp', 'mp')
- first_square_new: float32 [3, 3, 256, 256], P(None, None, 'dp', 'mp')
- second_mean_new: float32 [3, 3, 256, 256], P(None, None, 'dp', 'mp')
- second_square_new: float32 [3, 3, 256, 256], P(None, None, 'dp', 'mp')
- head_mean_new: float32 [2, 256, 601], P('mp', 'dp')
- head_square_new: float32 [2, 256, 601], P('mp', 'dp')
- embed_mean_new: float32 [2, 256], P('mp', 'dp')
- embed_square_new: float32 [2, 256], P('mp', 'dp')
- first_grad: float32 [3, 3, 256, 256], P(None, None, 'dp', 'mp')
- second_grad: float32 [3, 3, 256, 256], P(None, None, 'dp', 'mp')
- head_grad: float32 [2, 256, 601], P('mp', 'dp')
- embed_grad: float32 [2, 256], P('mp', 'dp')
Inputs may be any that keep to these rules, and one draw needn't show every extreme that they name: `actions`: the value 361 stands for a pass.
All inputs are finite; a program needn't handle non-finite values.
Results may differ from a plain program's by a relative error of at most 0.02.
Values may be sent and summed in bfloat16 or wider, within the bound.
No kernel may reach another device: no remote copies, remote signals or barrier semaphores. Data moves between devices by JAX's collectives and lax.ppermute only.
A program may use at most 64 MiB of HBM per device.

v0:
```python
import jax
import jax.numpy as jnp
from jax import lax
from jax.sharding import PartitionSpec as P

CHANNELS = 256
head_scale = 4.0
soft_cap = 15.0
eps_norm = 1e-05
beta_one = 0.9
beta_two = 0.999
step_size = 0.1
eps_adam = 1e-08


def conv_apply(field, kernel, layout):
    return lax.conv_general_dilated(
        field,
        kernel,
        (1, 1),
        "SAME",
        dimension_numbers=("NHWC", layout, "NHWC"),
        preferred_element_type=jnp.float32,
    )


def gate_slope(pre):
    sig = jax.nn.sigmoid(pre)
    return sig * (1.0 + pre * (1.0 - sig))


def tap_products(field, grad, field_rows):
    side = field.shape[1]
    padded = jnp.pad(field, ((0, 0), (1, 1), (1, 1), (0, 0)))
    flat_grad = grad.reshape(-1, grad.shape[3])
    blocks = []
    for offset in range(9):
        row_start = offset // 3
        col_start = offset % 3
        window = padded[:, row_start : row_start + side, col_start : col_start + side, :].reshape(
            -1, field.shape[3]
        )
        if field_rows:
            blocks.append(
                lax.dot_general(
                    window, flat_grad, (((0,), (0,)), ((), ())), preferred_element_type=jnp.float32
                )
            )
        else:
            blocks.append(
                lax.dot_general(
                    flat_grad, window, (((0,), (0,)), ((), ())), preferred_element_type=jnp.float32
                )
            )
    stacked = jnp.stack(blocks)
    return stacked.reshape(3, 3, stacked.shape[1], stacked.shape[2])


def action_planes(move, board):
    cells = board * board
    plane = (lax.broadcasted_iota(jnp.int32, (move.shape[0], cells), 1) == move[:, None]).astype(
        jnp.float32
    )
    passed = (move == cells).astype(jnp.float32)
    return (plane.reshape(move.shape[0], board, board, 1), passed[:, None, None, None])


def head_backward(state, head_used, value_now, reward_now, total):
    pooled = jnp.mean(state, axis=(1, 2)).astype(jnp.bfloat16)
    raw = head_scale * jnp.stack(
        [
            jnp.dot(pooled, head_used[0], preferred_element_type=jnp.float32),
            jnp.dot(pooled, head_used[1], preferred_element_type=jnp.float32),
        ]
    )
    squashed = jnp.tanh(raw / soft_cap)
    raised = jnp.exp(soft_cap * squashed)
    chances = raised / jnp.sum(raised, axis=2, keepdims=True)
    targets = jnp.stack([value_now, reward_now])
    picked = (lax.broadcasted_iota(jnp.int32, raw.shape, 2) == targets[:, :, None]).astype(
        jnp.float32
    )
    logit_grad = ((chances - picked) * (1.0 - squashed * squashed) / total).astype(jnp.bfloat16)
    pooled_grad = head_scale * (
        jnp.dot(logit_grad[0], head_used[0].T, preferred_element_type=jnp.float32)
        + jnp.dot(logit_grad[1], head_used[1].T, preferred_element_type=jnp.float32)
    )
    return (pooled, logit_grad, pooled_grad)


def adam_update(param, grad, mean, square):
    mean_new = beta_one * mean + (1.0 - beta_one) * grad
    square_new = beta_two * square + (1.0 - beta_two) * grad * grad
    param_new = param - step_size * mean_new / (jnp.sqrt(square_new) + eps_adam)
    return (param_new, mean_new, square_new)


def local(
    hidden_state,
    actions,
    value_target,
    reward_target,
    kernel_first,
    kernel_second,
    head_weight,
    action_embed,
    first_mean,
    first_square,
    second_mean,
    second_square,
    head_mean,
    head_square,
    embed_mean,
    embed_square,
):
    total = hidden_state.shape[0] * lax.axis_size("dp")
    board = hidden_state.shape[1]
    cells = board * board
    scale = (9.0 * CHANNELS) ** (-0.5)
    first_used, second_used, head_used, embed_used = (
        lax.all_gather(kernel_first.astype(jnp.bfloat16), "dp", axis=2, tiled=True),
        lax.all_gather(kernel_second.astype(jnp.bfloat16), "dp", axis=2, tiled=True),
        lax.all_gather(head_weight.astype(jnp.bfloat16), "dp", axis=1, tiled=True),
        lax.all_gather(action_embed.astype(jnp.bfloat16), "dp", axis=1, tiled=True),
    )
    first_used, second_used, head_used, embed_used = (
        lax.all_gather(first_used, "mp", axis=3, tiled=True),
        lax.all_gather(second_used, "mp", axis=3, tiled=True),
        lax.all_gather(head_used, "mp", axis=0, tiled=True),
        lax.all_gather(embed_used, "mp", axis=0, tiled=True),
    )
    count = hidden_state.shape[0] // lax.axis_size("mp")
    begin = lax.axis_index("mp") * count
    states = lax.dynamic_slice_in_dim(hidden_state, begin, count, 0)
    moves = lax.dynamic_slice_in_dim(actions, begin, count, 0)
    values = lax.dynamic_slice_in_dim(value_target, begin, count, 0)
    rewards = lax.dynamic_slice_in_dim(reward_target, begin, count, 0)
    unroll = moves.shape[1]
    embed = embed_used.astype(jnp.float32)
    state = states.astype(jnp.float32)
    saved = []
    for position in range(unroll):
        plane, passed = action_planes(moves[:, position], board)
        mixed = state + plane * embed[0] + passed * embed[1]
        conv_input = mixed.astype(jnp.bfloat16)
        pre = scale * conv_apply(conv_input, first_used, "HWIO")
        hidden = jax.nn.silu(pre).astype(jnp.bfloat16)
        branch = conv_apply(hidden, second_used, "HWOI")
        summed = mixed + scale * branch
        factor = lax.rsqrt(jnp.mean(summed * summed, axis=(1, 2, 3), keepdims=True) + eps_norm)
        state = summed * factor
        pooled, logit_grad, pooled_grad = head_backward(
            state, head_used, values[:, position], rewards[:, position], total
        )
        saved.append(
            (
                plane,
                passed,
                conv_input,
                pre,
                hidden,
                summed,
                factor,
                pooled,
                logit_grad,
                pooled_grad,
            )
        )
    first_grad = jnp.zeros(first_used.shape, jnp.float32)
    second_grad = jnp.zeros(second_used.shape, jnp.float32)
    head_grad = jnp.zeros(head_used.shape, jnp.float32)
    embed_grad = jnp.zeros(embed_used.shape, jnp.float32)
    carry = jnp.zeros(states.shape, jnp.float32)
    for position in range(unroll - 1, -1, -1):
        plane, passed, conv_input, pre, hidden, summed, factor, pooled, logit_grad, pooled_grad = (
            saved[position]
        )
        state_grad = carry + pooled_grad[:, None, None, :] / cells
        summed_grad = factor * state_grad - factor * factor * factor * summed * jnp.mean(
            state_grad * summed, axis=(1, 2, 3), keepdims=True
        )
        branch_grad = summed_grad.astype(jnp.bfloat16)
        hidden_grad = scale * conv_apply(branch_grad, second_used[::-1, ::-1], "HWIO")
        inner_grad = (hidden_grad * gate_slope(pre)).astype(jnp.bfloat16)
        input_grad = conv_apply(inner_grad, first_used[::-1, ::-1], "HWOI")
        carry = summed_grad + scale * input_grad
        first_grad = first_grad + scale * tap_products(conv_input, inner_grad, True)
        second_grad = second_grad + scale * tap_products(hidden, branch_grad, False)
        head_grad = head_grad + head_scale * jnp.stack(
            [
                lax.dot_general(
                    pooled,
                    logit_grad[0],
                    (((0,), (0,)), ((), ())),
                    preferred_element_type=jnp.float32,
                ),
                lax.dot_general(
                    pooled,
                    logit_grad[1],
                    (((0,), (0,)), ((), ())),
                    preferred_element_type=jnp.float32,
                ),
            ]
        )
        embed_grad = embed_grad + jnp.stack(
            [jnp.sum(plane * carry, axis=(0, 1, 2)), jnp.sum(passed * carry, axis=(0, 1, 2))]
        )
    first_grad, second_grad, head_grad, embed_grad = (
        lax.psum_scatter(first_grad, "mp", scatter_dimension=3, tiled=True),
        lax.psum_scatter(second_grad, "mp", scatter_dimension=3, tiled=True),
        lax.psum_scatter(head_grad, "mp", scatter_dimension=0, tiled=True),
        lax.psum_scatter(embed_grad, "mp", scatter_dimension=0, tiled=True),
    )
    first_grad, second_grad, head_grad, embed_grad = (
        lax.psum_scatter(first_grad, "dp", scatter_dimension=2, tiled=True),
        lax.psum_scatter(second_grad, "dp", scatter_dimension=2, tiled=True),
        lax.psum_scatter(head_grad, "dp", scatter_dimension=1, tiled=True),
        lax.psum_scatter(embed_grad, "dp", scatter_dimension=1, tiled=True),
    )
    first_new, first_mean_new, first_square_new = adam_update(
        kernel_first, first_grad, first_mean, first_square
    )
    second_new, second_mean_new, second_square_new = adam_update(
        kernel_second, second_grad, second_mean, second_square
    )
    head_new, head_mean_new, head_square_new = adam_update(
        head_weight, head_grad, head_mean, head_square
    )
    embed_new, embed_mean_new, embed_square_new = adam_update(
        action_embed, embed_grad, embed_mean, embed_square
    )
    return (
        first_new,
        second_new,
        head_new,
        embed_new,
        first_mean_new,
        first_square_new,
        second_mean_new,
        second_square_new,
        head_mean_new,
        head_square_new,
        embed_mean_new,
        embed_square_new,
        first_grad,
        second_grad,
        head_grad,
        embed_grad,
    )


def solution(mesh):
    placed = (
        P("dp", None, None, None),
        P("dp", None),
        P("dp", None),
        P("dp", None),
        P(None, None, "dp", "mp"),
        P(None, None, "dp", "mp"),
        P("mp", "dp", None),
        P("mp", "dp"),
        P(None, None, "dp", "mp"),
        P(None, None, "dp", "mp"),
        P(None, None, "dp", "mp"),
        P(None, None, "dp", "mp"),
        P("mp", "dp", None),
        P("mp", "dp", None),
        P("mp", "dp"),
        P("mp", "dp"),
    )
    return jax.shard_map(
        local,
        mesh=mesh,
        in_specs=placed,
        out_specs=(
            P(None, None, "dp", "mp"),
            P(None, None, "dp", "mp"),
            P("mp", "dp", None),
            P("mp", "dp"),
            P(None, None, "dp", "mp"),
            P(None, None, "dp", "mp"),
            P(None, None, "dp", "mp"),
            P(None, None, "dp", "mp"),
            P("mp", "dp", None),
            P("mp", "dp", None),
            P("mp", "dp"),
            P("mp", "dp"),
            P(None, None, "dp", "mp"),
            P(None, None, "dp", "mp"),
            P("mp", "dp", None),
            P("mp", "dp"),
        ),
        check_vma=False,
    )
```

profile of v0, /device:TPU:0, one launch (start us, length us, event | category | flops | bytes accessed | tf_op | source)
XLA Modules:
  0.0 581.1 jit_solution(16968905555778703401)
XLA Ops:
  7.3 1.0 convert_element_type.150
  8.3 48.3 %all_gather.26 = bf16[3,3,256,128]{3,2,1,0:T(8,128)(2,1)} all-gather(bf16[3,3,16,128]{3,2,1,0:T(8,128)(2,1)S(1)} %convert_element_type.150), channel_id=1, replica_groups=mesh['dp'=16,'mp'=2] {'dp'}, dimensions={2}, use_global_device_ids=true | all-gather | bytes 626688 | tf_op jit(solution)/shard_map/all_gather | solution.py:121
  56.6 0.9 convert_element_type.152
  57.5 41.0 %all_gather.28 = bf16[3,3,256,128]{3,2,1,0:T(8,128)(2,1)} all-gather(bf16[3,3,16,128]{3,2,1,0:T(8,128)(2,1)S(1)} %convert_element_type.152), channel_id=1, replica_groups=mesh['dp'=16,'mp'=2] {'dp'}, dimensions={2}, use_global_device_ids=true | all-gather | bytes 626688 | tf_op jit(solution)/shard_map/all_gather | solution.py:122
  98.6 0.6 dynamic-slice
  100.1 38.8 %all-reduce.4 = bf16[256]{0:T(256)(128)(2,1)S(1)} all-reduce(bf16[256]{0:T(256)(128)(2,1)S(1)} %dynamic-update-slice), channel_id=1, replica_groups=mesh['dp'=16,'mp'=2] {'dp'}, use_global_device_ids=true, to_apply=%add.4 | all-reduce | flops 256 | bytes 1024
  138.9 1.8 all-gather
  140.8 0.6 fusion.358
  142.6 0.7 fusion.265
  143.7 0.7 fusion.266
  144.4 37.2 %all_gather.30 = bf16[1,256,601]{2,1,0:T(8,128)(2,1)S(1)} all-gather(bf16[1,16,601]{2,1,0:T(8,128)(2,1)S(1)} %convert_element_type.157), channel_id=1, replica_groups=mesh['dp'=16,'mp'=2] {'dp'}, dimensions={1}, use_global_device_ids=true | all-gather | bytes 326944 | tf_op jit(solution)/shard_map/all_gather | solution.py:123
  181.6 0.6 fusion.356
  183.4 1.4 add_reduce_fusion
  184.8 1.4 add_reduce_fusion.1
  186.2 2.4 all_gather.31
  188.6 0.8 fusion.61
  189.5 2.0 fusion.6
  192.3 2.0 convolution_multiply_fusion.3
  194.8 0.8 multiply_reduce_fusion.8
  196.4 0.7 copy-done.1
  197.4 2.1 fusion.5
  199.5 0.8 select_bitcast_fusion.2
  200.4 0.8 convolution_multiply_fusion.2
  201.7 0.8 multiply_reduce_fusion.7
  205.3 0.7 multiply_reduce_fusion.5
  206.8 0.7 fusion.126
  207.8 2.1 fusion.7
  210.6 0.8 convolution_multiply_fusion.1
  211.9 0.8 multiply_reduce_fusion.3
  213.3 0.8 fusion.348
  214.2 1.0 pad.29
  215.3 0.7 slice.243
  216.4 1.2 fusion
  218.3 1.2 fusion.17
  219.6 1.2 fusion.16
  220.8 1.3 fusion.15
  222.1 1.2 fusion.14
  223.4 1.2 fusion.13
  224.6 1.2 fusion.12
  225.9 1.2 fusion.11
  227.1 1.3 fusion.10
  228.4 1.2 fusion.9
  229.8 0.9 reshape.830
  230.6 1.0 slice_bitcast_fusion.9
  231.6 1.2 fusion.26
  235.6 2.0 add_multiply_fusion
  237.7 0.8 copy-done.8
  238.7 2.0 fusion.8
  247.1 1.7 add_multiply_fusion.1
  250.2 0.8 convolution_multiply_fusion
  251.8 2.5 all-reduce.5
  254.2 0.7 constant_dynamic-slice_fusion.4
  254.9 0.8 copy.106
  255.8 0.7 reduce-scatter.20.cloned.1.call-update
  256.5 0.7 reduce-scatter.16.cloned.1.call-update
  257.3 1.5 reduce-scatter.10.cloned.1.call-done
  258.8 80.4 %reduce-scatter.22.cloned.1.call-done = f32[16,1]{1,0:T(8,128)} async-done(((f32[256,1]{1,0:T(8,128)}), f32[16,1]{1,0:T(8,128)}) %reduce-scatter.22.cloned.1.call-update) | async-done | bytes 80
  339.2 0.8 copy.107
  340.5 75.6 %reduce-scatter.20.cloned.1.call-done = f32[1,16,601]{2,1,0:T(8,128)} async-done(((f32[1,256,601]{2,1,0:T(8,128)}), f32[1,16,601]{2,1,0:T(8,128)}) %reduce-scatter.20.cloned.1.call-update) | async-done | bytes 38480 | tf_op jit(solution)/shard_map/reduce_scatter | solution.py:217
  416.1 1.4 divide_subtract_fusion.2
  417.6 77.1 %reduce-scatter.16.cloned.1.call-done = f32[3,3,16,128]{3,2,1,0:T(8,128)} async-done(((f32[3,3,256,128]{3,2,1,0:T(8,128)}), f32[3,3,16,128]{3,2,1,0:T(8,128)}) %reduce-scatter.16.cloned.1.call-update) | async-done | bytes 73744 | tf_op jit(solution)/shard_map/reduce_scatter | solution.py:216
  494.6 1.6 divide_subtract_fusion
  496.2 76.8 %reduce-scatter.12.cloned.1.call-done = f32[3,3,16,128]{3,2,1,0:T(8,128)} async-done(((f32[3,3,256,128]{3,2,1,0:T(8,128)}), f32[3,3,16,128]{3,2,1,0:T(8,128)}) %reduce-scatter.12.cloned.1.call-update) | async-done | bytes 73744 | tf_op jit(solution)/shard_map/reduce_scatter | solution.py:215
  573.0 1.6 divide_subtract_fusion.1
  (206 shorter events, 20.9 us)
Async XLA Ops:
  7.2 136.1 %copy-start = (bf16[2,19,19,256]{3,0,2,1:T(2,128)(2,1)S(1)}, bf16[2,19,19,256]{3,0,2,1:T(2,128)(2,1)}, u32[]{:S(2)}) copy-start(bf16[2,19,19,256]{3,0,2,1:T(2,128)(2,1)} %param.16) | copy-start | bytes 1108996
  7.2 91.4 %copy-start.38 = (u32[32]{0:T(128)S(1)}, u32[32]{0:T(128)}, u32[]{:S(2)}) copy-start(u32[32]{0:T(128)} %constant.145) | copy-start | bytes 388
  7.2 91.4 %copy-start.28 = (f32[1,16]{1,0:T(1,128)S(1)}, f32[1,16]{1,0:T(1,128)}, u32[]{:S(2)}) copy-start(f32[1,16]{1,0:T(1,128)} %param.23) | copy-start | bytes 196
  7.2 133.5 %copy-start.36 = (s32[2,2]{1,0:T(2,128)S(1)}, s32[2,2]{1,0:T(2,128)}, u32[]{:S(2)}) copy-start(s32[2,2]{1,0:T(2,128)} %param.17) | copy-start | bytes 52
  7.2 137.1 %copy-start.17 = (f32[1,16,601]{2,1,0:T(8,128)S(1)}, f32[1,16,601]{2,1,0:T(8,128)}, u32[]{:S(2)}) copy-start(f32[1,16,601]{2,1,0:T(8,128)} %param.22) | copy-start | bytes 115396
  7.2 174.4 %copy-start.32 = (s32[2,2]{1,0:T(2,128)S(1)}, s32[2,2]{1,0:T(2,128)}, u32[]{:S(2)}) copy-start(s32[2,2]{1,0:T(2,128)} %param.18) | copy-start | bytes 52
  7.3 174.4 %copy-start.31 = (s32[2,2]{1,0:T(2,128)S(1)}, s32[2,2]{1,0:T(2,128)}, u32[]{:S(2)}) copy-start(s32[2,2]{1,0:T(2,128)} %param.19) | copy-start | bytes 52
  7.3 182.2 %all-gather.4.cloned.1.call-start = ((), (), s32[]{:S(2)}) async-start(), calls=%async_computation.7 | async-start | bytes 1769472 | tf_op jit(solution)/shard_map/all_gather | solution.py:127
  56.6 135.1 %all-gather.6.cloned.1.call-start = ((), (), s32[]{:S(2)}) async-start(), calls=%async_computation.8 | async-start | bytes 1769472 | tf_op jit(solution)/shard_map/all_gather | solution.py:128
  98.5 157.2 %reduce-scatter.18.cloned.1.call-start = ((), (), s32[]{:S(2)}) async-start(), calls=%async_computation.13 | async-start | bytes 1966080 | tf_op jit(solution)/shard_map/reduce_scatter | solution.py:211
  181.6 7.9 %copy-start.26 = (pred[8,3]{0,1:T(4,128)(4,1)S(1)}, pred[8,3]{0,1:T(4,128)(4,1)}, u32[]{:S(2)}) copy-start(pred[8,3]{0,1:T(4,128)(4,1)} %constant.135) | copy-start | bytes 76
  191.5 0.8 copy-start.9
  196.4 0.7 copy-start.1
  197.4 3.0 copy-start.35
  199.5 0.9 copy-start.11
  204.5 3.3 copy-start.12
  207.8 2.8 copy-start.33
  209.9 0.7 copy-start.5
  215.3 2.3 copy-start.7
  217.7 38.8 %reduce-scatter.14.cloned.1.call-start = ((), (), s32[]{:S(2)}) async-start(), calls=%async_computation.11 | async-start | bytes 3538944 | tf_op jit(solution)/shard_map/reduce_scatter | solution.py:210
  227.1 2.5 copy-start.3
  230.6 2.2 copy-start.16
  233.2 0.9 copy-start.4
  237.6 0.9 copy-start.8
  237.6 1.1 copy-start.10
  237.6 1.2 copy-start.19
  237.6 3.1 copy-start.6
  237.6 3.8 copy-start.15
  237.6 21.2 %reduce-scatter.10.cloned.1.call-start = ((), (), s32[]{:S(2)}) async-start(), calls=%async_computation.9 | async-start | bytes 3538944 | tf_op jit(solution)/shard_map/reduce_scatter | solution.py:209
  243.5 1.0 copy-start.2
  248.8 0.7 copy-start.37
  248.8 1.4 copy-start.34
  248.9 90.3 %reduce-scatter.22.cloned.1.call-start = ((), (), s32[]{:S(2)}) async-start(), calls=%async_computation.15 | async-start | bytes 139264
  251.5 88.5 %copy-start.29 = (f32[1,16]{1,0:T(1,128)S(1)}, f32[1,16]{1,0:T(1,128)}, u32[]{:S(2)}) copy-start(f32[1,16]{1,0:T(1,128)} %param.30) | copy-start | bytes 196
  251.5 88.5 %copy-start.30 = (f32[1,16]{1,0:T(1,128)S(1)}, f32[1,16]{1,0:T(1,128)}, u32[]{:S(2)}) copy-start(f32[1,16]{1,0:T(1,128)} %param.31) | copy-start | bytes 196
  251.5 164.7 %copy-start.18 = (f32[1,16,601]{2,1,0:T(8,128)S(1)}, f32[1,16,601]{2,1,0:T(8,128)}, u32[]{:S(2)}) copy-start(f32[1,16,601]{2,1,0:T(8,128)} %param.22) | copy-start | bytes 115396
  251.5 164.6 %copy-start.24 = (f32[1,16,601]{2,1,0:T(8,128)S(1)}, f32[1,16,601]{2,1,0:T(8,128)}, u32[]{:S(2)}) copy-start(f32[1,16,601]{2,1,0:T(8,128)} %param.28) | copy-start | bytes 115396
  251.5 164.6 %copy-start.25 = (f32[1,16,601]{2,1,0:T(8,128)S(1)}, f32[1,16,601]{2,1,0:T(8,128)}, u32[]{:S(2)}) copy-start(f32[1,16,601]{2,1,0:T(8,128)} %param.29) | copy-start | bytes 115396
  251.5 243.1 %copy-start.13 = (f32[3,3,16,128]{3,2,1,0:T(8,128)S(1)}, f32[3,3,16,128]{3,2,1,0:T(8,128)}, u32[]{:S(2)}) copy-start(f32[3,3,16,128]{3,2,1,0:T(8,128)} %param.21) | copy-start | bytes 221188
  251.5 243.1 %copy-start.20 = (f32[3,3,16,128]{3,2,1,0:T(8,128)S(1)}, f32[3,3,16,128]{3,2,1,0:T(8,128)}, u32[]{:S(2)}) copy-start(f32[3,3,16,128]{3,2,1,0:T(8,128)} %param.26) | copy-start | bytes 221188
  251.5 243.1 %copy-start.21 = (f32[3,3,16,128]{3,2,1,0:T(8,128)S(1)}, f32[3,3,16,128]{3,2,1,0:T(8,128)}, u32[]{:S(2)}) copy-start(f32[3,3,16,128]{3,2,1,0:T(8,128)} %param.27) | copy-start | bytes 221188
  251.5 321.5 %copy-start.14 = (f32[3,3,16,128]{3,2,1,0:T(8,128)S(1)}, f32[3,3,16,128]{3,2,1,0:T(8,128)}, u32[]{:S(2)}) copy-start(f32[3,3,16,128]{3,2,1,0:T(8,128)} %param.20) | copy-start | bytes 221188
  251.6 321.5 %copy-start.22 = (f32[3,3,16,128]{3,2,1,0:T(8,128)S(1)}, f32[3,3,16,128]{3,2,1,0:T(8,128)}, u32[]{:S(2)}) copy-start(f32[3,3,16,128]{3,2,1,0:T(8,128)} %param.24) | copy-start | bytes 221188
  251.6 321.4 %copy-start.23 = (f32[3,3,16,128]{3,2,1,0:T(8,128)S(1)}, f32[3,3,16,128]{3,2,1,0:T(8,128)}, u32[]{:S(2)}) copy-start(f32[3,3,16,128]{3,2,1,0:T(8,128)} %param.25) | copy-start | bytes 221188
  255.7 160.4 %reduce-scatter.20.cloned.1.call-start = ((), (), s32[]{:S(2)}) async-start(), calls=%async_computation.14 | async-start | bytes 696320 | tf_op jit(solution)/shard_map/reduce_scatter | solution.py:217
  256.5 238.2 %reduce-scatter.16.cloned.1.call-start = ((), (), s32[]{:S(2)}) async-start(), calls=%async_computation.12 | async-start | bytes 1253376 | tf_op jit(solution)/shard_map/reduce_scatter | solution.py:216
  257.2 315.8 %reduce-scatter.12.cloned.1.call-start = ((), (), s32[]{:S(2)}) async-start(), calls=%async_computation.10 | async-start | bytes 1253376 | tf_op jit(solution)/shard_map/reduce_scatter | solution.py:215
  340.0 234.7 %copy-start.27 = (f32[1,16]{1,0:T(1,128)}, f32[1,16]{1,0:T(1,128)S(1)}, u32[]{:S(2)}) copy-start(f32[1,16]{1,0:T(1,128)S(1)} %copy.107) | copy-start | bytes 196
Sparse Core Ops, SparseCore 0:
  56.7 4.7 all-gather.3
  98.7 6.9 all-gather.5
  217.8 6.4 reduce-scatter.17
  237.7 7.6 reduce-scatter.13
  249.0 9.7 reduce-scatter.9
  260.9 78.2 reduce-scatter.21
  342.0 74.0 reduce-scatter.19
  419.0 75.6 reduce-scatter.15
  497.5 75.4 reduce-scatter.11
where the time goes:
time: 582 us; the launch traced here: 581 us
  waiting for transfers between devices  313 us (54%)
  blocking collectives  172 us (30%)
  matrix products  33.7 us (6%)
  other arithmetic  24.3 us (4%)
  between operations  19.6 us (3%)
  local copies, waits for them, and re-layouts  18.2 us (3%)
    unnamed x10, waiting for transfers between devices  81.8 us
    reduce_scatter x1, waiting for transfers between devices, local(): lax.psum_scatter(second_grad, 'dp', scatter_dimension=2, tiled=True)  77.1 us
    reduce_scatter x1, waiting for transfers between devices, local(): lax.psum_scatter(first_grad, 'dp', scatter_dimension=2, tiled=True)  76.8 us
    reduce_scatter x1, waiting for transfers between devices, local(): lax.psum_scatter(head_grad, 'dp', scatter_dimension=1, tiled=True)  75.6 us
    all_gather x1, blocking collectives, local(): lax.all_gather(kernel_first.astype(jnp.bfloat16), 'dp', axis=2, tiled=True)  48.3 us
    unnamed x2, blocking collectives  41.3 us
    all_gather x1, blocking collectives, local(): lax.all_gather(kernel_second.astype(jnp.bfloat16), 'dp', axis=2, tiled=True)  41 us
    all_gather x1, blocking collectives, local(): lax.all_gather(head_weight.astype(jnp.bfloat16), 'dp', axis=1, tiled=True)  37.2 us
  transfers between devices with their start and end apart: 9, of which 5 were waited for; matrix products, arithmetic and copies ran while one was open for 8% of the time, Pallas kernels for 0%

commit v1 on v0

--- a/solution.py
+++ b/solution.py
@@ -11,6 +11,20 @@
 beta_two = 0.999
 step_size = 0.1
 eps_adam = 1e-08
+
+
+def take_runs(block_in):
+    how_many = jax.lax.axis_size("dp")
+    frames = tuple(((ii, (ii + 1) % how_many) for ii in range(how_many)))
+    blocks_here = tuple(((ii, (ii - 1) % how_many) for ii in range(how_many)))
+    main, wide_out = ([block_in], [block_in])
+    for _ in range(how_many // 2):
+        main.append(jax.lax.ppermute(main[-1], "dp", frames))
+    for _ in range((how_many - 1) // 2):
+        even = jax.lax.ppermute(wide_out[-1], "dp", blocks_here)
+        wide_out.append(even)
+    n_now = jnp.concatenate([*main[::-1], *wide_out[1:]], 1)
+    return jnp.roll(n_now, (jax.lax.axis_index("dp") - how_many // 2) * block_in.shape[1], 1)
 
 
 def conv_apply(field, kernel, layout):
@@ -120,7 +134,7 @@
     first_used, second_used, head_used, embed_used = (
         lax.all_gather(kernel_first.astype(jnp.bfloat16), "dp", axis=2, tiled=True),
         lax.all_gather(kernel_second.astype(jnp.bfloat16), "dp", axis=2, tiled=True),
-        lax.all_gather(head_weight.astype(jnp.bfloat16), "dp", axis=1, tiled=True),
+        take_runs(head_weight.astype(jnp.bfloat16)),
         lax.all_gather(action_embed.astype(jnp.bfloat16), "dp", axis=1, tiled=True),
     )
     first_used, second_used, head_used, embed_used = (

time: 582 us -> 615 us (1.057)
  starting transfers between devices: 0.59 us -> 41.6 us
  blocking collectives: 172 us -> 135 us
  waiting for transfers between devices: 313 us -> 333 us
  local copies, waits for them, and re-layouts: 18.2 us -> 27.4 us
    ppermute x0 -> x15, starting transfers between devices: none -> 41 us  [the longest x7 40.4 us: take_runs(): even = jax.lax.ppermute(wide_out[-1], 'dp', blocks_here)]
    all_gather x1 -> x0, blocking collectives: 37.2 us -> none  [local(): lax.all_gather(head_weight.astype(jnp.bfloat16), 'dp', axis=1, tiled=True)]
    ppermute x0 -> x15, waiting for transfers between devices: none -> 21.5 us  [the longest x8 20.9 us: take_runs(): main.append(jax.lax.ppermute(main[-1], 'dp', frames))]
    concatenate x0 -> x1, local copies, waits for them, and re-layouts: none -> 7.64 us  [take_runs(): jnp.roll(n_now, (jax.lax.axis_index('dp') - how_many // 2) * block_in.sha...]
  transfers between devices with their start and end apart: 9 -> 24, of which waited for: 5 -> 14; matrix products, arithmetic and copies ran while one was open for 8% -> 9% of each run, Pallas kernels for 0% -> 0%
where the time goes in v1:
time: 615 us; the launch traced here: 614 us
  waiting for transfers between devices  333 us (54%)
  blocking collectives  135 us (22%)
  starting transfers between devices  41.6 us (7%)
  matrix products  33.8 us (5%)
  local copies, waits for them, and re-layouts  27.4 us (4%)
  other arithmetic  24.2 us (4%)
  between operations  19.7 us (3%)
    unnamed x10, waiting for transfers between devices  81.6 us
    reduce_scatter x1, waiting for transfers between devices, local(): lax.psum_scatter(first_grad, 'dp', scatter_dimension=2, tiled=True)  76.9 us
    reduce_scatter x1, waiting for transfers between devices, local(): lax.psum_scatter(second_grad, 'dp', scatter_dimension=2, tiled=True)  76.7 us
    reduce_scatter x1, waiting for transfers between devices, local(): lax.psum_scatter(head_grad, 'dp', scatter_dimension=1, tiled=True)  75.7 us
    all_gather x1, blocking collectives, local(): lax.all_gather(kernel_first.astype(jnp.bfloat16), 'dp', axis=2, tiled=True)  48.4 us
    all_gather x1, blocking collectives, local(): lax.all_gather(kernel_second.astype(jnp.bfloat16), 'dp', axis=2, tiled=True)  41.5 us
    unnamed x2, blocking collectives  40.6 us
    ppermute x7, starting transfers between devices, take_runs(): even = jax.lax.ppermute(wide_out[-1], 'dp', blocks_here)  40.4 us
  transfers between devices with their start and end apart: 24, of which 14 were waited for; matrix products, arithmetic and copies ran while one was open for 9% of the time, Pallas kernels for 0%

profile of v1, /device:TPU:0, one launch (start us, length us, event | category | flops | bytes accessed | tf_op | source)
XLA Modules:
  0.0 614.1 jit_solution(11987569932995698358)
XLA Ops:
  7.3 0.9 convert_element_type.150
  8.2 48.4 %all_gather.23 = bf16[3,3,256,128]{3,2,1,0:T(8,128)(2,1)} all-gather(bf16[3,3,16,128]{3,2,1,0:T(8,128)(2,1)S(1)} %convert_element_type.150), channel_id=1, replica_groups=mesh['dp'=16,'mp'=2] {'dp'}, dimensions={2}, use_global_device_ids=true | all-gather | bytes 626688 | tf_op jit(solution)/shard_map/all_gather | solution.py:135
  56.7 0.9 copy.77
  57.7 5.6 collective-permute-start.8
  63.3 0.9 convert_element_type.152
  64.2 41.5 %all_gather.25 = bf16[3,3,256,128]{3,2,1,0:T(8,128)(2,1)} all-gather(bf16[3,3,16,128]{3,2,1,0:T(8,128)(2,1)S(1)} %convert_element_type.152), channel_id=1, replica_groups=mesh['dp'=16,'mp'=2] {'dp'}, dimensions={2}, use_global_device_ids=true | all-gather | bytes 626688 | tf_op jit(solution)/shard_map/all_gather | solution.py:136
  109.3 38.1 %all-reduce.4 = bf16[256]{0:T(256)(128)(2,1)S(1)} all-reduce(bf16[256]{0:T(256)(128)(2,1)S(1)} %dynamic-update-slice), channel_id=1, replica_groups=mesh['dp'=16,'mp'=2] {'dp'}, use_global_device_ids=true, to_apply=%add.4 | all-reduce | flops 256 | bytes 1024
  147.4 1.8 all-gather
  150.9 5.2 collective-permute-start.9
  156.2 4.0 collective-permute-done.1
  160.1 0.8 fusion.61
  161.0 5.6 collective-permute-start.10
  166.6 2.4 collective-permute-done.2
  169.7 5.9 collective-permute-start.11
  175.5 2.4 collective-permute-done.3
  178.3 6.1 collective-permute-start.12
  184.4 2.4 collective-permute-done.4
  187.4 5.8 collective-permute-start.13
  193.2 2.4 collective-permute-done.5
  196.0 6.2 %collective-permute-start.14 = (bf16[1,16,601]{1,2,0:T(8,128)(2,1)}, bf16[1,16,601]{1,2,0:T(8,128)(2,1)}, u32[]{:S(2)}, u32[]{:S(2)}) collective-permute-start(bf16[1,16,601]{1,2,0:T(8,128)(2,1)} %collective-permute-done.13), channel_id=1, source_target_pairs={{0,30},{2,0},{4,2},{6,4},{8,6},{10,8},{12,10},{14,12},{16,14},{18,... | collective-permute-start | bytes 57704 | tf_op jit(solution)/shard_map/ppermute | solution.py:24
  202.2 2.4 collective-permute-done.6
  206.1 2.7 add_reduce_fusion
  208.9 4.9 collective-permute-done.7
  213.7 7.6 %concatenate.30 = bf16[1,512,601]{1,2,0:T(8,128)(2,1)S(1)} concatenate(bf16[1,16,601]{1,2,0:T(8,128)(2,1)} %collective-permute-done.7, bf16[1,16,601]{1,2,0:T(8,128)(2,1)} %collective-permute-done.6, bf16[1,16,601]{1,2,0:T(8,128)(2,1)} %copy-done.9, bf16[1,16,601]{1,2,0:T(8,128)(2,1)S(1)} %collective-permute-done.4, bf16[1,16,601]{1,2,0:T(8,128)(2,1)S(1)} %collective-permute-done.3, ...), dimensions={1} | concatenate | bytes 1230848 | tf_op jit(solution)/shard_map/jit(_roll_dynamic)/concatenate | solution.py:27
  221.6 2.4 all_gather.27
  224.0 2.1 fusion.6
  226.9 2.0 convolution_multiply_fusion.3
  229.4 0.8 multiply_reduce_fusion.8
  232.0 2.1 fusion.5
  234.1 0.9 select_bitcast_fusion.2
  236.3 0.8 multiply_reduce_fusion.7
  242.5 2.1 fusion.7
  245.3 0.8 convolution_multiply_fusion.1
  246.5 0.8 multiply_reduce_fusion.3
  248.0 0.8 fusion.348
  248.8 1.0 pad.29
  251.1 1.2 fusion
  253.0 1.2 fusion.17
  254.2 1.3 fusion.16
  255.6 1.2 fusion.15
  256.8 1.2 fusion.14
  258.1 1.2 fusion.13
  259.3 1.2 fusion.12
  260.5 1.2 fusion.11
  261.8 1.3 fusion.10
  263.0 1.2 fusion.9
  264.4 0.9 reshape.830
  265.3 1.0 slice_bitcast_fusion.9
  266.3 1.2 fusion.26
  270.3 2.0 add_multiply_fusion
  272.4 0.8 copy-done.8
  273.4 2.0 fusion.8
  281.8 1.8 add_multiply_fusion.1
  284.9 0.8 convolution_multiply_fusion
  286.5 2.5 all-reduce.5
  289.6 0.8 copy.88
  292.7 79.7 %reduce-scatter.22.cloned.1.call-done = f32[16,1]{1,0:T(8,128)} async-done(((f32[256,1]{1,0:T(8,128)}), f32[16,1]{1,0:T(8,128)}) %reduce-scatter.22.cloned.1.call-update) | async-done | bytes 80
  372.4 0.8 copy.89
  373.7 75.7 %reduce-scatter.20.cloned.1.call-done = f32[1,16,601]{2,1,0:T(8,128)} async-done(((f32[1,256,601]{2,1,0:T(8,128)}), f32[1,16,601]{2,1,0:T(8,128)}) %reduce-scatter.20.cloned.1.call-update) | async-done | bytes 38480 | tf_op jit(solution)/shard_map/reduce_scatter | solution.py:231
  449.4 1.4 divide_subtract_fusion.2
  450.9 76.7 %reduce-scatter.16.cloned.1.call-done = f32[3,3,16,128]{3,2,1,0:T(8,128)} async-done(((f32[3,3,256,128]{3,2,1,0:T(8,128)}), f32[3,3,16,128]{3,2,1,0:T(8,128)}) %reduce-scatter.16.cloned.1.call-update) | async-done | bytes 73744 | tf_op jit(solution)/shard_map/reduce_scatter | solution.py:230
  527.5 1.6 divide_subtract_fusion
  529.1 76.9 %reduce-scatter.12.cloned.1.call-done = f32[3,3,16,128]{3,2,1,0:T(8,128)} async-done(((f32[3,3,256,128]{3,2,1,0:T(8,128)}), f32[3,3,16,128]{3,2,1,0:T(8,128)}) %reduce-scatter.12.cloned.1.call-update) | async-done | bytes 73744 | tf_op jit(solution)/shard_map/reduce_scatter | solution.py:229
  606.0 1.6 divide_subtract_fusion.1
  (236 shorter events, 32.1 us)
Async XLA Ops:
  7.2 142.0 %copy-start = (bf16[2,19,19,256]{3,0,2,1:T(2,128)(2,1)S(1)}, bf16[2,19,19,256]{3,0,2,1:T(2,128)(2,1)}, u32[]{:S(2)}) copy-start(bf16[2,19,19,256]{3,0,2,1:T(2,128)(2,1)} %param.16) | copy-start | bytes 1108996
  7.2 100.6 %copy-start.38 = (u32[32]{0:T(128)S(1)}, u32[32]{0:T(128)}, u32[]{:S(2)}) copy-start(u32[32]{0:T(128)} %constant.175) | copy-start | bytes 388
  7.2 98.6 %copy-start.34 = (s32[2,2]{1,0:T(2,128)S(1)}, s32[2,2]{1,0:T(2,128)}, u32[]{:S(2)}) copy-start(s32[2,2]{1,0:T(2,128)} %param.17) | copy-start | bytes 52
  7.2 100.5 %copy-start.28 = (f32[1,16]{1,0:T(1,128)S(1)}, f32[1,16]{1,0:T(1,128)}, u32[]{:S(2)}) copy-start(f32[1,16]{1,0:T(1,128)} %param.23) | copy-start | bytes 196
  7.2 216.8 %all-gather.4.cloned.1.call-start = ((), (), s32[]{:S(2)}) async-start(), calls=%async_computation.7 | async-start | bytes 1769472 | tf_op jit(solution)/shard_map/all_gather | solution.py:141
  8.2 169.7 %copy-start.35 = (s32[2,2]{1,0:T(2,128)S(1)}, s32[2,2]{1,0:T(2,128)}, u32[]{:S(2)}) copy-start(s32[2,2]{1,0:T(2,128)} %param.18) | copy-start | bytes 52
  8.2 187.5 %copy-start.36 = (s32[2,2]{1,0:T(2,128)S(1)}, s32[2,2]{1,0:T(2,128)}, u32[]{:S(2)}) copy-start(s32[2,2]{1,0:T(2,128)} %param.19) | copy-start | bytes 52
  56.7 169.7 %all-gather.6.cloned.1.call-start = ((), (), s32[]{:S(2)}) async-start(), calls=%async_computation.8 | async-start | bytes 1769472 | tf_op jit(solution)/shard_map/all_gather | solution.py:142
  57.7 92.6 %collective-permute-start = (bf16[1,16,601]{1,2,0:T(8,128)(2,1)S(1)}, bf16[1,16,601]{1,2,0:T(8,128)(2,1)S(1)}, u32[]{:S(2)}, u32[]{:S(2)}) collective-permute-start(bf16[1,16,601]{1,2,0:T(8,128)(2,1)S(1)} %copy.77), channel_id=1, source_target_pairs={{0,2},{2,4},{4,6},{6,8},{8,10},{10,12},{12,14},{14,16},{16,18},{18... | collective-permute-start | bytes 57704 | tf_op jit(solution)/shard_map/ppermute | solution.py:22
  57.7 93.2 %collective-permute-start.8 = (bf16[1,16,601]{1,2,0:T(8,128)(2,1)S(1)}, bf16[1,16,601]{1,2,0:T(8,128)(2,1)S(1)}, u32[]{:S(2)}, u32[]{:S(2)}) collective-permute-start(bf16[1,16,601]{1,2,0:T(8,128)(2,1)S(1)} %copy.77), channel_id=1, source_target_pairs={{0,30},{2,0},{4,2},{6,4},{8,6},{10,8},{12,10},{14,12},{16,14},{18,... | collective-permute-start | bytes 57704 | tf_op jit(solution)/shard_map/ppermute | solution.py:24
  105.8 184.8 %reduce-scatter.18.cloned.1.call-start = ((), (), s32[]{:S(2)}) async-start(), calls=%async_computation.13 | async-start | bytes 1966080 | tf_op jit(solution)/shard_map/reduce_scatter | solution.py:225
  150.3 9.8 %collective-permute-start.1 = (bf16[1,16,601]{1,2,0:T(8,128)(2,1)S(1)}, bf16[1,16,601]{1,2,0:T(8,128)(2,1)S(1)}, u32[]{:S(2)}, u32[]{:S(2)}) collective-permute-start(bf16[1,16,601]{1,2,0:T(8,128)(2,1)S(1)} %collective-permute-done), channel_id=1, source_target_pairs={{0,2},{2,4},{4,6},{6,8},{8,10},{10,12},{12,14},{14,16},{16,18},{18... | collective-permute-start | bytes 57704 | tf_op jit(solution)/shard_map/ppermute | solution.py:22
  150.9 10.0 %collective-permute-start.9 = (bf16[1,16,601]{1,2,0:T(8,128)(2,1)S(1)}, bf16[1,16,601]{1,2,0:T(8,128)(2,1)S(1)}, u32[]{:S(2)}, u32[]{:S(2)}) collective-permute-start(bf16[1,16,601]{1,2,0:T(8,128)(2,1)S(1)} %collective-permute-done.8), channel_id=1, source_target_pairs={{0,30},{2,0},{4,2},{6,4},{8,6},{10,8},{12,10},{14,12},{16,14},{18,... | collective-permute-start | bytes 57704 | tf_op jit(solution)/shard_map/ppermute | solution.py:24
  160.1 8.8 %collective-permute-start.2 = (bf16[1,16,601]{1,2,0:T(8,128)(2,1)S(1)}, bf16[1,16,601]{1,2,0:T(8,128)(2,1)S(1)}, u32[]{:S(2)}, u32[]{:S(2)}) collective-permute-start(bf16[1,16,601]{1,2,0:T(8,128)(2,1)S(1)} %collective-permute-done.1), channel_id=1, source_target_pairs={{0,2},{2,4},{4,6},{6,8},{8,10},{10,12},{12,14},{14,16},{16,18},{18... | collective-permute-start | bytes 57704 | tf_op jit(solution)/shard_map/ppermute | solution.py:22
  161.0 8.7 %collective-permute-start.10 = (bf16[1,16,601]{1,2,0:T(8,128)(2,1)S(1)}, bf16[1,16,601]{1,2,0:T(8,128)(2,1)S(1)}, u32[]{:S(2)}, u32[]{:S(2)}) collective-permute-start(bf16[1,16,601]{1,2,0:T(8,128)(2,1)S(1)} %collective-permute-done.9), channel_id=1, source_target_pairs={{0,30},{2,0},{4,2},{6,4},{8,6},{10,8},{12,10},{14,12},{16,14},{18,... | collective-permute-start | bytes 57704 | tf_op jit(solution)/shard_map/ppermute | solution.py:24
  169.0 8.9 %collective-permute-start.3 = (bf16[1,16,601]{1,2,0:T(8,128)(2,1)S(1)}, bf16[1,16,601]{1,2,0:T(8,128)(2,1)S(1)}, u32[]{:S(2)}, u32[]{:S(2)}) collective-permute-start(bf16[1,16,601]{1,2,0:T(8,128)(2,1)S(1)} %collective-permute-done.2), channel_id=1, source_target_pairs={{0,2},{2,4},{4,6},{6,8},{8,10},{10,12},{12,14},{14,16},{16,18},{18... | collective-permute-start | bytes 57704 | tf_op jit(solution)/shard_map/ppermute | solution.py:22
  169.7 8.6 %collective-permute-start.11 = (bf16[1,16,601]{1,2,0:T(8,128)(2,1)S(1)}, bf16[1,16,601]{1,2,0:T(8,128)(2,1)S(1)}, u32[]{:S(2)}, u32[]{:S(2)}) collective-permute-start(bf16[1,16,601]{1,2,0:T(8,128)(2,1)S(1)} %collective-permute-done.10), channel_id=1, source_target_pairs={{0,30},{2,0},{4,2},{6,4},{8,6},{10,8},{12,10},{14,12},{16,14},{18,... | collective-permute-start | bytes 57704 | tf_op jit(solution)/shard_map/ppermute | solution.py:24
  177.9 8.9 %collective-permute-start.4 = (bf16[1,16,601]{1,2,0:T(8,128)(2,1)S(1)}, bf16[1,16,601]{1,2,0:T(8,128)(2,1)S(1)}, u32[]{:S(2)}, u32[]{:S(2)}) collective-permute-start(bf16[1,16,601]{1,2,0:T(8,128)(2,1)S(1)} %collective-permute-done.3), channel_id=1, source_target_pairs={{0,2},{2,4},{4,6},{6,8},{8,10},{10,12},{12,14},{14,16},{16,18},{18... | collective-permute-start | bytes 57704 | tf_op jit(solution)/shard_map/ppermute | solution.py:22
  178.3 9.1 %collective-permute-start.12 = (bf16[1,16,601]{1,2,0:T(8,128)(2,1)S(1)}, bf16[1,16,601]{1,2,0:T(8,128)(2,1)S(1)}, u32[]{:S(2)}, u32[]{:S(2)}) collective-permute-start(bf16[1,16,601]{1,2,0:T(8,128)(2,1)S(1)} %collective-permute-done.11), channel_id=1, source_target_pairs={{0,30},{2,0},{4,2},{6,4},{8,6},{10,8},{12,10},{14,12},{16,14},{18,... | collective-permute-start | bytes 57704 | tf_op jit(solution)/shard_map/ppermute | solution.py:24
  186.8 8.8 %collective-permute-start.5 = (bf16[1,16,601]{1,2,0:T(8,128)(2,1)S(1)}, bf16[1,16,601]{1,2,0:T(8,128)(2,1)S(1)}, u32[]{:S(2)}, u32[]{:S(2)}) collective-permute-start(bf16[1,16,601]{1,2,0:T(8,128)(2,1)S(1)} %collective-permute-done.4), channel_id=1, source_target_pairs={{0,2},{2,4},{4,6},{6,8},{8,10},{10,12},{12,14},{14,16},{16,18},{18... | collective-permute-start | bytes 57704 | tf_op jit(solution)/shard_map/ppermute | solution.py:22
  187.4 8.6 %collective-permute-start.13 = (bf16[1,16,601]{1,2,0:T(8,128)(2,1)S(1)}, bf16[1,16,601]{1,2,0:T(8,128)(2,1)}, u32[]{:S(2)}, u32[]{:S(2)}) collective-permute-start(bf16[1,16,601]{1,2,0:T(8,128)(2,1)S(1)} %collective-permute-done.12), channel_id=1, source_target_pairs={{0,30},{2,0},{4,2},{6,4},{8,6},{10,8},{12,10},{14,12},{16,14},{18,... | collective-permute-start | bytes 57704 | tf_op jit(solution)/shard_map/ppermute | solution.py:24
  195.7 9.6 %copy-start.9 = (bf16[1,16,601]{1,2,0:T(8,128)(2,1)}, bf16[1,16,601]{1,2,0:T(8,128)(2,1)S(1)}, u32[]{:S(2)}) copy-start(bf16[1,16,601]{1,2,0:T(8,128)(2,1)S(1)} %collective-permute-done.5) | copy-start | bytes 57700
  195.7 8.9 %collective-permute-start.6 = (bf16[1,16,601]{1,2,0:T(8,128)(2,1)S(1)}, bf16[1,16,601]{1,2,0:T(8,128)(2,1)}, u32[]{:S(2)}, u32[]{:S(2)}) collective-permute-start(bf16[1,16,601]{1,2,0:T(8,128)(2,1)S(1)} %collective-permute-done.5), channel_id=1, source_target_pairs={{0,2},{2,4},{4,6},{6,8},{8,10},{10,12},{12,14},{14,16},{16,18},{18... | collective-permute-start | bytes 57704 | tf_op jit(solution)/shard_map/ppermute | solution.py:22
  196.0 12.9 %collective-permute-start.14 = (bf16[1,16,601]{1,2,0:T(8,128)(2,1)}, bf16[1,16,601]{1,2,0:T(8,128)(2,1)}, u32[]{:S(2)}, u32[]{:S(2)}) collective-permute-start(bf16[1,16,601]{1,2,0:T(8,128)(2,1)} %collective-permute-done.13), channel_id=1, source_target_pairs={{0,30},{2,0},{4,2},{6,4},{8,6},{10,8},{12,10},{14,12},{16,14},{18,... | collective-permute-start | bytes 57704 | tf_op jit(solution)/shard_map/ppermute | solution.py:24
  204.6 9.1 %collective-permute-start.7 = (bf16[1,16,601]{1,2,0:T(8,128)(2,1)}, bf16[1,16,601]{1,2,0:T(8,128)(2,1)}, u32[]{:S(2)}, u32[]{:S(2)}) collective-permute-start(bf16[1,16,601]{1,2,0:T(8,128)(2,1)} %collective-permute-done.6), channel_id=1, source_target_pairs={{0,2},{2,4},{4,6},{6,8},{8,10},{10,12},{12,14},{14,16},{16,18},{18... | collective-permute-start | bytes 57704 | tf_op jit(solution)/shard_map/ppermute | solution.py:22
  208.9 15.1 %copy-start.26 = (pred[8,3]{0,1:T(4,128)(4,1)S(1)}, pred[8,3]{0,1:T(4,128)(4,1)}, u32[]{:S(2)}) copy-start(pred[8,3]{0,1:T(4,128)(4,1)} %constant.165) | copy-start | bytes 76
  226.1 0.8 copy-start.10
  231.0 0.7 copy-start.1
  232.0 3.0 copy-start.33
  234.1 0.9 copy-start.12
  239.1 3.3 copy-start.13
  242.5 2.8 copy-start.31
  244.6 0.7 copy-start.5
  250.0 2.3 copy-start.7
  252.3 38.9 %reduce-scatter.14.cloned.1.call-start = ((), (), s32[]{:S(2)}) async-start(), calls=%async_computation.11 | async-start | bytes 3538944 | tf_op jit(solution)/shard_map/reduce_scatter | solution.py:224
  261.8 2.5 copy-start.3
  265.3 2.2 copy-start.17
  267.8 0.9 copy-start.4
  272.3 0.9 copy-start.8
  272.3 1.1 copy-start.11
  272.3 1.2 copy-start.19
  272.3 3.2 copy-start.6
  272.3 3.9 copy-start.16
  272.3 19.9 %reduce-scatter.10.cloned.1.call-start = ((), (), s32[]{:S(2)}) async-start(), calls=%async_computation.9 | async-start | bytes 3538944 | tf_op jit(solution)/shard_map/reduce_scatter | solution.py:223
  278.2 1.0 copy-start.2
  283.6 0.7 copy-start.37
  283.6 1.4 copy-start.32
  283.6 88.8 %reduce-scatter.22.cloned.1.call-start = ((), (), s32[]{:S(2)}) async-start(), calls=%async_computation.15 | async-start | bytes 139264
  286.2 87.0 %copy-start.29 = (f32[1,16]{1,0:T(1,128)S(1)}, f32[1,16]{1,0:T(1,128)}, u32[]{:S(2)}) copy-start(f32[1,16]{1,0:T(1,128)} %param.30) | copy-start | bytes 196
  286.2 87.0 %copy-start.30 = (f32[1,16]{1,0:T(1,128)S(1)}, f32[1,16]{1,0:T(1,128)}, u32[]{:S(2)}) copy-start(f32[1,16]{1,0:T(1,128)} %param.31) | copy-start | bytes 196
  286.2 163.2 %copy-start.18 = (f32[1,16,601]{2,1,0:T(8,128)S(1)}, f32[1,16,601]{2,1,0:T(8,128)}, u32[]{:S(2)}) copy-start(f32[1,16,601]{2,1,0:T(8,128)} %param.22) | copy-start | bytes 115396
  286.2 163.2 %copy-start.24 = (f32[1,16,601]{2,1,0:T(8,128)S(1)}, f32[1,16,601]{2,1,0:T(8,128)}, u32[]{:S(2)}) copy-start(f32[1,16,601]{2,1,0:T(8,128)} %param.28) | copy-start | bytes 115396
  286.2 163.2 %copy-start.25 = (f32[1,16,601]{2,1,0:T(8,128)S(1)}, f32[1,16,601]{2,1,0:T(8,128)}, u32[]{:S(2)}) copy-start(f32[1,16,601]{2,1,0:T(8,128)} %param.29) | copy-start | bytes 115396
  286.2 241.3 %copy-start.14 = (f32[3,3,16,128]{3,2,1,0:T(8,128)S(1)}, f32[3,3,16,128]{3,2,1,0:T(8,128)}, u32[]{:S(2)}) copy-start(f32[3,3,16,128]{3,2,1,0:T(8,128)} %param.21) | copy-start | bytes 221188
  286.3 241.3 %copy-start.20 = (f32[3,3,16,128]{3,2,1,0:T(8,128)S(1)}, f32[3,3,16,128]{3,2,1,0:T(8,128)}, u32[]{:S(2)}) copy-start(f32[3,3,16,128]{3,2,1,0:T(8,128)} %param.26) | copy-start | bytes 221188
  286.3 241.3 %copy-start.21 = (f32[3,3,16,128]{3,2,1,0:T(8,128)S(1)}, f32[3,3,16,128]{3,2,1,0:T(8,128)}, u32[]{:S(2)}) copy-start(f32[3,3,16,128]{3,2,1,0:T(8,128)} %param.27) | copy-start | bytes 221188
  286.3 319.7 %copy-start.15 = (f32[3,3,16,128]{3,2,1,0:T(8,128)S(1)}, f32[3,3,16,128]{3,2,1,0:T(8,128)}, u32[]{:S(2)}) copy-start(f32[3,3,16,128]{3,2,1,0:T(8,128)} %param.20) | copy-start | bytes 221188
  286.3 319.7 %copy-start.22 = (f32[3,3,16,128]{3,2,1,0:T(8,128)S(1)}, f32[3,3,16,128]{3,2,1,0:T(8,128)}, u32[]{:S(2)}) copy-start(f32[3,3,16,128]{3,2,1,0:T(8,128)} %param.24) | copy-start | bytes 221188
  286.3 319.7 %copy-start.23 = (f32[3,3,16,128]{3,2,1,0:T(8,128)S(1)}, f32[3,3,16,128]{3,2,1,0:T(8,128)}, u32[]{:S(2)}) copy-start(f32[3,3,16,128]{3,2,1,0:T(8,128)} %param.25) | copy-start | bytes 221188
  290.4 159.0 %reduce-scatter.20.cloned.1.call-start = ((), (), s32[]{:S(2)}) async-start(), calls=%async_computation.14 | async-start | bytes 696320 | tf_op jit(solution)/shard_map/reduce_scatter | solution.py:231
  291.2 236.3 %reduce-scatter.16.cloned.1.call-start = ((), (), s32[]{:S(2)}) async-start(), calls=%async_computation.12 | async-start | bytes 1253376 | tf_op jit(solution)/shard_map/reduce_scatter | solution.py:230
  291.9 314.0 %reduce-scatter.12.cloned.1.call-start = ((), (), s32[]{:S(2)}) async-start(), calls=%async_computation.10 | async-start | bytes 1253376 | tf_op jit(solution)/shard_map/reduce_scatter | solution.py:229
  373.2 234.4 %copy-start.27 = (f32[1,16]{1,0:T(1,128)}, f32[1,16]{1,0:T(1,128)S(1)}, u32[]{:S(2)}) copy-start(f32[1,16]{1,0:T(1,128)S(1)} %copy.89) | copy-start | bytes 196
Sparse Core Ops, SparseCore 0:
  56.8 4.7 all-gather.3
  105.9 6.2 all-gather.5
  252.5 5.2 reduce-scatter.17
  272.4 6.3 reduce-scatter.13
  283.7 8.4 reduce-scatter.9
  294.3 78.0 reduce-scatter.21
  375.2 74.1 reduce-scatter.19
  452.3 75.2 reduce-scatter.15
  530.4 75.5 reduce-scatter.11
